TPU v7x, 32 devices: a whole 2x2x4 slice. The times are simulated.
32 devices in a mesh: section: 4 (over x, core), wide: 8 (over z, y).
Axes of the slice: x: 2, y: 2, z: 4, core: 2. Of those that a mesh axis runs over, the one named last changes fastest.
Arguments:
- stream: bfloat16 [4, 512, 2048], P('section', 'wide'), may hold values from -3 to 3
- mixer_gain: float32 [4, 2048], P('section'), may hold values from 0.1 to 1.9
- ssm_weight: bfloat16 [4, 2048, 160], P('section'), may hold values from -0.125 to 0.125
- decay_rate: float32 [4, 32], P('section'), may hold values from 9.765625e-05 to 0.04
- skip_gain: float32 [4, 32], P('section'), may hold values from 0.5 to 1.5
- mixed_gain: float32 [4, 2048], P('section'), may hold values from 0.1 to 1.9
- ffn_gain: float32 [4, 2048], P('section'), may hold values from 0.1 to 1.9
- router_weight: bfloat16 [4, 2048, 4], P('section'), may hold values from -0.125 to 0.125
- expert_ids: int32 [4, 512, 2], P('section', 'wide'), may hold values from 0 to 3, all different within a row; in each aligned block of 64 rows (0 to 63, 64 to 127, ..., all dimensions but the last counted through in order) at most 40 rows name the same one
- gate_weight: bfloat16 [4, 2048, 28672], P('section', None, 'wide'), may hold values from -0.125 to 0.125
- up_weight: bfloat16 [4, 2048, 28672], P('section', None, 'wide'), may hold values from -0.125 to 0.125
- down_weight: bfloat16 [4, 28672, 2048], P('section', 'wide'), may hold values from -0.0625 to 0.0625
Outputs:
- carried: bfloat16 [4, 512, 2048], P('section', 'wide')
Inputs may be any that keep to these rules, and one draw needn't show every extreme that they name: `expert_ids`: A token's 2 experts differ. Among the tokens of one device, no expert is named by more than 40 of them, a bound that some block reaches.
All inputs are finite; a program needn't handle non-finite values.
Results may differ from a plain program's by a relative error of at most 0.0085.
Values may be sent and summed in bfloat16 or wider, within the bound.
A program may use at most 128 MiB of HBM per device.

v0:
```python
import functools
import math

import jax
import jax.numpy as jnp
from jax import lax
from jax.experimental import pallas as pl
from jax.experimental.pallas import tpu as pltpu
from jax.sharding import PartitionSpec as P

STATE = 64
EXPERTS = 4
CAP = 40
EPSILON = 1e-05
PIECES = 8
VMEM_BYTES = 67_000_000
F32 = jnp.float32
BF16 = jnp.bfloat16


def tile_of(extent, most):
    return max(t for t in range(128, most + 1, 128) if extent % t == 0)


def rms_scale(values, gain_row):
    mean_sq = jnp.mean(values * values, axis=-1, keepdims=True)
    return values * lax.rsqrt(mean_sq + EPSILON) * gain_row


def iota(shape, axis):
    return lax.broadcasted_iota(jnp.int32, shape, axis)


def dot(a, b):
    return jnp.dot(a, b, preferred_element_type=F32)


def tick(
    sections,
    n,
    stream,
    mixer_gain,
    ssm_weight,
    decay_rate,
    skip_gain,
    mixed_gain,
    ffn_gain,
    router_weight,
    expert_ids,
    gate_hbm,
    up_hbm,
    down_hbm,
    out_ref,
    gate,
    up,
    down,
    stage,
    maps,
    cum,
    read_out,
    read_in,
    mixed,
    resid,
    notes,
    resid_in,
    notes_in,
    packed,
    arrived,
    rows_in,
    hidden,
    answers,
    answers_in,
    picked,
    w_sem,
    maps_send,
    maps_recv,
    read_send,
    read_recv,
    pass_send,
    pass_recv,
    rows_send,
    rows_recv,
    ans_send,
    ans_recv,
):
    sec = lax.axis_index("section")
    me = lax.axis_index("wide")
    after = lax.rem(sec + 1, sections)
    before = lax.rem(sec + sections - 1, sections)
    tok, width = stream.shape
    heads = decay_rate.shape[1]
    head_dim = width // heads
    chans = width // n
    local_heads = chans // head_dim
    total = n * tok
    members = n // EXPERTS
    my_expert, my_part = me // members, lax.rem(me, members)
    hid = gate.shape[1]
    order = [0]
    for k in range(1, n // 2 + 1):
        order += [k] if 2 * k == n else [k, n - k]

    def wide_at(shift):
        return lax.rem(me + (shift + n), n)

    def peer(shift, part_shift):
        expert = lax.rem(my_expert + (shift + EXPERTS), EXPERTS)
        return expert * members + lax.rem(my_part + (part_shift + members), members)

    def remote(src, dst, send, recv, section, wide):
        return pltpu.make_async_remote_copy(
            src_ref=src,
            dst_ref=dst,
            send_sem=send,
            recv_sem=recv,
            device_id={"section": section, "wide": wide},
            device_id_type=pl.DeviceIdType.MESH,
        )

    barrier = pltpu.get_barrier_semaphore()
    for k in range(n):
        w = wide_at(k)
        if k:
            pl.semaphore_signal(
                barrier, inc=1, device_id={"section": sec, "wide": w},
                device_id_type=pl.DeviceIdType.MESH,
            )
        for other in (after, before):
            pl.semaphore_signal(
                barrier, inc=1, device_id={"section": other, "wide": w},
                device_id_type=pl.DeviceIdType.MESH,
            )

    weight_copies = []
    for i, (src, dst) in enumerate(((gate_hbm, gate), (up_hbm, up), (down_hbm, down))):
        step = src.shape[0] // PIECES
        weight_copies.append(
            [
                pltpu.make_async_copy(
                    src.at[pl.ds(k * step, step)], dst.at[pl.ds(k * step, step)], w_sem.at[i, k]
                )
                for k in range(PIECES)
            ]
        )
        for copy in weight_copies[-1]:
            copy.start()

    x_in = stream[...].astype(F32)
    normed = rms_scale(x_in, mixer_gain[...]).astype(BF16)
    projected = lax.dot_general(
        normed, ssm_weight[...], (((1,), (1,)), ((), ())), preferred_element_type=F32
    )
    raw = projected[:, 2 * STATE :]
    step_size = jnp.maximum(raw, 0.0) + jnp.log1p(jnp.exp(-jnp.abs(raw)))
    high = step_size.astype(BF16).astype(F32)
    steps = jnp.concatenate(
        [high, step_size - high, jnp.zeros((tok, 128 - 2 * heads), F32)], axis=1
    ).astype(BF16)
    bc = projected[:, : 2 * STATE].astype(BF16)
    for j in range(n):
        stage[j, :, 0:128] = bc
        stage[j, :, 128:256] = steps
        stage[j, :, 256:] = normed[:, j * chans : (j + 1) * chans]

    pl.semaphore_wait(barrier, 3 * n - 1)
    maps_own = pltpu.make_async_copy(stage.at[me], maps.at[me], maps_recv.at[me])
    maps_own.start()
    for p in reversed(range(1, n)):
        w = wide_at(order[p])
        remote(stage.at[w], maps.at[me], maps_send.at[w], maps_recv.at[me], sec, w).start()
    spread = (iota((heads, width), 1) // head_dim == iota((heads, width), 0)).astype(F32)
    skip_cols = jnp.dot(
        skip_gain[...], spread, precision=lax.Precision.HIGHEST, preferred_element_type=F32
    )
    mixed[...] = normed.astype(F32) * skip_cols
    rates = [
        jnp.sum(
            jnp.where(iota((1, heads), 1) == me * local_heads + j, decay_rate[...], 0.0),
            axis=1,
            keepdims=True,
        )
        for j in range(local_heads)
    ]
    maps_own.wait()
    for p in range(1, n):
        w = wide_at(order[p])
        remote(stage.at[w], maps.at[w], maps_send.at[w], maps_recv.at[w], sec, w).wait()

    both = maps[:, :, 0:128].reshape(total, 128)
    parts = maps[:, :, 128:256].reshape(total, 128)
    values = maps[:, :, 256:].reshape(total, chans)
    rows128, cols128 = iota((128, 128), 0), iota((128, 128), 1)
    c_all = dot(both, (rows128 == cols128 + STATE).astype(BF16)).astype(BF16)
    head_at = me * local_heads + iota((128, chans), 1) // head_dim
    row_at = iota((128, chans), 0)
    step_cols = dot(parts, ((row_at == head_at) | (row_at == head_at + heads)).astype(BF16))
    scaled = values.astype(F32) * step_cols
    chan_head = iota((total, chans), 1) // head_dim
    per_head = [
        jnp.where(chan_head == j, scaled, 0.0).astype(BF16) for j in range(local_heads)
    ]
    mine = (cols128 < local_heads) & (rows128 == me * local_heads + cols128)
    mine_low = (cols128 < local_heads) & (rows128 == heads + me * local_heads + cols128)
    high_own = dot(parts, mine.astype(BF16)).astype(BF16)
    low_own = dot(parts, mine_low.astype(BF16)).astype(BF16)
    for r in range(n):
        span = (r + 1) * tok
        tri = (r * tok + iota((tok, span), 0) >= iota((tok, span), 1)).astype(BF16)
        cum[r * tok : span, :] = dot(tri, high_own[:span]) + dot(tri, low_own[:span])
    cum_rows = jnp.transpose(cum[...])
    for r in range(n):
        span = (r + 1) * tok
        seen = r * tok + iota((tok, span), 0) >= iota((tok, span), 1)
        overlap = lax.dot_general(
            c_all[r * tok : span], both[:span], (((1,), (1,)), ((), ())),
            preferred_element_type=F32,
        ) * (1.0 / (STATE * math.sqrt(STATE)))
        total_out = None
        for j in range(local_heads):
            gap = rates[j] * (cum_rows[j : j + 1, :span] - cum[r * tok : span, j : j + 1])
            mixing = (overlap * jnp.exp(jnp.where(seen, gap, -1e30))).astype(BF16)
            part = dot(mixing, per_head[j][:span])
            total_out = part if total_out is None else total_out + part
        read_out[r] = total_out.astype(BF16)
    read_own = pltpu.make_async_copy(read_out.at[me], read_in.at[me], read_recv.at[me])
    read_own.start()
    for p in reversed(range(1, n)):
        w = wide_at(order[p])
        remote(read_out.at[w], read_in.at[me], read_send.at[w], read_recv.at[me], sec, w).start()

    id_rows = jnp.concatenate([expert_ids[...], jnp.zeros((6, tok), jnp.int32)], axis=0)
    ids = jnp.transpose(id_rows.astype(F32)).astype(jnp.int32)
    id0, id1 = ids[:, 0:1], ids[:, 1:2]
    lane = iota((tok, 128), 1)
    chosen = ((lane == id0) | (lane == id1)).astype(BF16)
    earlier = (iota((tok, tok), 0) > iota((tok, tok), 1)).astype(BF16)
    running = dot(earlier, chosen)
    slot0 = jnp.sum(jnp.where(lane == id0, running, 0.0), axis=1, keepdims=True)
    slot1 = jnp.sum(jnp.where(lane == id1, running, 0.0), axis=1, keepdims=True)
    target0 = id0.astype(F32) * CAP + slot0
    target1 = id1.astype(F32) * CAP + slot1
    places = iota((tok, 256), 1).astype(F32)
    placing = jnp.transpose(((places == target0) | (places == target1)).astype(F32)).astype(BF16)

    read_own.wait()
    for p in range(1, n):
        w = wide_at(order[p])
        remote(read_out.at[w], read_in.at[w], read_send.at[w], read_recv.at[w], sec, w).wait()
    for j in range(n):
        at = slice(j * chans, (j + 1) * chans)
        mixed[:, at] = mixed[:, at] + read_in[j].astype(F32)
    residual = x_in + rms_scale(mixed[...], mixed_gain[...])
    routed = rms_scale(residual, ffn_gain[...]).astype(BF16)
    sent = dot(placing[: EXPERTS * CAP], routed)
    for e in range(EXPERTS):
        packed[e] = sent[e * CAP : (e + 1) * CAP].astype(BF16)

    rows_own = pltpu.make_async_copy(packed.at[my_expert], arrived.at[0], rows_recv.at[0])
    rows_own.start()
    far_first = sorted(range(EXPERTS), key=lambda q: -min(q, EXPERTS - q))
    row_copies = {}
    for q in far_first[:-1]:
        w = peer(-q, 0)
        row_copies[q] = remote(
            packed.at[w // members], arrived.at[q], rows_send.at[q], rows_recv.at[q], sec, w
        )
        row_copies[q].start()

    def hand_on(q):
        block = arrived.at[q] if q else packed.at[my_expert]
        for k in range(1, members):
            p = k * EXPERTS + q
            row_copies[p] = remote(
                block, arrived.at[p], rows_send.at[p], rows_recv.at[p], sec, peer(0, -k)
            )
            row_copies[p].start()

    hand_on(0)

    logits = lax.dot_general(
        routed, router_weight[...], (((1,), (1,)), ((), ())), preferred_element_type=F32
    )
    choice = iota((tok, EXPERTS), 1)
    logit0 = jnp.sum(jnp.where(choice == id0, logits, 0.0), axis=1, keepdims=True)
    logit1 = jnp.sum(jnp.where(choice == id1, logits, 0.0), axis=1, keepdims=True)
    share0 = jax.nn.sigmoid(logit0 - logit1)
    resid[...] = residual
    notes[...] = jnp.where(
        lane == 0, target0, jnp.where(lane == 1, target1, jnp.where(lane == 2, share0, 0.0))
    )
    passes = [
        remote(resid, resid_in, pass_send.at[0], pass_recv.at[0], after, me),
        remote(notes, notes_in, pass_send.at[1], pass_recv.at[1], after, me),
    ]
    for copy in passes:
        copy.start()

    for q in reversed(far_first[:-1]):
        row_copies[q].wait_recv()
        hand_on(q)

    half = n // 2
    hid_tile = tile_of(hid, 512)
    out_tile = tile_of(width, 512)
    answer_copies = {}
    for group in range(2):
        slots = range(group * half, (group + 1) * half)
        for p in slots:
            if p == 0:
                rows_own.wait()
            elif p >= EXPERTS:
                row_copies[p].wait_recv()
        for q, p in enumerate(slots):
            if q % 2 == 0:
                rows_in[q * CAP : (q + 2) * CAP] = jnp.concatenate(
                    [arrived[p].astype(F32), arrived[p + 1].astype(F32)], axis=0
                ).astype(BF16)
        if group == 0:
            for copies in weight_copies[:2]:
                for copy in copies:
                    copy.wait()

        @pl.loop(0, hid // hid_tile)
        def _(i):
            at = pl.ds(pl.multiple_of(i * hid_tile, hid_tile), hid_tile)
            gate_pre = dot(rows_in[...], gate[:, at])
            up_pre = dot(rows_in[...], up[:, at])
            hidden[:, at] = (gate_pre * jax.nn.sigmoid(gate_pre) * up_pre).astype(BF16)

        if group == 0:
            for copy in weight_copies[2]:
                copy.wait()

        @pl.loop(0, width // out_tile)
        def _(i):
            at = pl.ds(pl.multiple_of(i * out_tile, out_tile), out_tile)
            result = dot(hidden[...], down[:, at])
            for q in range(half):
                answers[group * half + q, :, at] = result[q * CAP : (q + 1) * CAP].astype(BF16)

        for p in sorted(slots, key=lambda p: far_first.index(p % EXPERTS)):
            answer_copies[p] = remote(
                answers.at[p], answers_in.at[p], ans_send.at[p], ans_recv.at[p], after,
                peer(p % EXPERTS, p // EXPERTS),
            )
            answer_copies[p].start()

    for copy in passes:
        copy.wait()
    told = notes_in[...]
    goal0, goal1, first_share = told[:, 0:1], told[:, 1:2], told[:, 2:3]
    slot_lane = iota((tok, CAP), 1)
    for p in range(n):
        base = (peer(-(p % EXPERTS), 0) // members) * CAP
        spots = (slot_lane + base).astype(F32)
        take = jnp.concatenate(
            [(spots == goal0).astype(F32), (spots == goal1).astype(F32)], axis=0
        ).astype(BF16)
        answer_copies[p].wait_recv()
        found = dot(take, answers_in[p])
        if p == 0:
            picked[...] = found
        elif p < n - 1:
            picked[...] += found
        else:
            found = picked[...] + found
            out_ref[...] = (
                resid_in[...] + (first_share * found[:tok] + (1.0 - first_share) * found[tok:])
            ).astype(BF16)
    for p in range(1, n):
        row_copies[p].wait_send()
    for p in range(n):
        answer_copies[p].wait_send()


def local(
    stream,
    mixer_gain,
    ssm_weight,
    decay_rate,
    skip_gain,
    mixed_gain,
    ffn_gain,
    router_weight,
    expert_ids,
    gate_weight,
    up_weight,
    down_weight,
):
    n = lax.axis_size("wide")
    sections = lax.axis_size("section")
    _, tok, width = stream.shape
    hid = gate_weight.shape[2]
    chans = width // n
    dma = pltpu.SemaphoreType.DMA
    vmem = pl.BlockSpec(memory_space=pltpu.VMEM)
    hbm = pl.BlockSpec(memory_space=pl.ANY)
    result = pl.pallas_call(
        functools.partial(tick, sections, n),
        out_shape=jax.ShapeDtypeStruct((tok, width), BF16),
        in_specs=[vmem] * 9 + [hbm] * 3,
        out_specs=vmem,
        scratch_shapes=[
            pltpu.VMEM((width, hid), BF16),
            pltpu.VMEM((width, hid), BF16),
            pltpu.VMEM((hid, width), BF16),
            pltpu.VMEM((n, tok, 256 + chans), BF16),
            pltpu.VMEM((n, tok, 256 + chans), BF16),
            pltpu.VMEM((n * tok, 128), F32),
            pltpu.VMEM((n, tok, chans), BF16),
            pltpu.VMEM((n, tok, chans), BF16),
            pltpu.VMEM((tok, width), F32),
            pltpu.VMEM((tok, width), F32),
            pltpu.VMEM((tok, 128), F32),
            pltpu.VMEM((tok, width), F32),
            pltpu.VMEM((tok, 128), F32),
            pltpu.VMEM((EXPERTS, CAP, width), BF16),
            pltpu.VMEM((n, CAP, width), BF16),
            pltpu.VMEM((n // 2 * CAP, width), BF16),
            pltpu.VMEM((n // 2 * CAP, hid), BF16),
            pltpu.VMEM((n, CAP, width), BF16),
            pltpu.VMEM((n, CAP, width), BF16),
            pltpu.VMEM((2 * tok, width), F32),
            dma((3, PIECES)),
            dma((n,)),
            dma((n,)),
            dma((n,)),
            dma((n,)),
            dma((2,)),
            dma((2,)),
            dma((n,)),
            dma((n,)),
            dma((n,)),
            dma((n,)),
        ],
        compiler_params=pltpu.CompilerParams(
            collective_id=0, has_side_effects=True, vmem_limit_bytes=VMEM_BYTES
        ),
    )(
        stream[0],
        mixer_gain,
        ssm_weight[0].T,
        decay_rate,
        skip_gain,
        mixed_gain,
        ffn_gain,
        router_weight[0].T,
        expert_ids[0].T,
        gate_weight[0],
        up_weight[0],
        down_weight[0],
    )
    return result[None]


def solution(mesh):
    return jax.shard_map(
        local,
        mesh=mesh,
        in_specs=(
            P("section", "wide", None),
            P("section", None),
            P("section", None, None),
            P("section", None),
            P("section", None),
            P("section", None),
            P("section", None),
            P("section", None, None),
            P("section", "wide", None),
            P("section", None, "wide"),
            P("section", None, "wide"),
            P("section", "wide", None),
        ),
        out_specs=P("section", "wide", None),
        check_vma=False,
    )
```

profile of v0, /device:TPU:1, one launch (start us, length us, event | category | flops | bytes accessed | tf_op | source)
XLA Modules:
  0.0 82.8 jit_solution(13112238619558663930)
XLA Ops:
  0.0 81.1 %shard_map.118 = bf16[64,2048]{1,0:T(8,128)(2,1)} custom-call(bf16[64,2048]{1,0:T(8,128)(2,1)} %bitcast.19, f32[1,2048]{1,0:T(1,128)} %mixer_gain.1, bf16[160,2048]{1,0:T(8,128)(2,1)} %bitcast.18, f32[1,32]{1,0:T(1,128)} %decay_rate.1, f32[1,32]{1,0:T(1,128)} %skip_gain.1, f32[1,2048]{1,0:T(1,128)} %mixed_gain.1, f32[1,2048]{1,0:T(1,128)} %ffn_gain.1, ...), custom_call_target="tpu_custom_call" | custom-call | tf_op jit(solution)/shard_map/pallas_call | solution.py:398
  81.2 1.7 %copy.14 = bf16[1,64,2048]{2,1,0:T(8,128)(2,1)} copy(bf16[1,64,2048]{2,1,0:T(8,128)(2,1)} %bitcast.17) | data formatting | bytes 524288
where the time goes:
time: 84.5 us; the launch traced here: 82.8 us
  Pallas kernels  81.1 us (96%)
  local copies, waits for them, and re-layouts  1.67 us (2%)
    pallas_call x1, Pallas kernels, local(): pl.pallas_call(functools.partial(tick, sections, n), out_shape=jax.ShapeD...  81.1 us

commit v1 on v0

v1 whole, which is shorter than its diff:
```python
import functools
import math

import jax
import jax.numpy as jnp
from jax import lax
from jax.experimental import pallas as pl
from jax.experimental.pallas import tpu as pltpu
from jax.sharding import PartitionSpec as P

STATE = 64
EXPERTS = 4
CAP = 40
EPSILON = 1e-05
PIECES = 8
CUTS = 2
VMEM_BYTES = 67_000_000
F32 = jnp.float32
BF16 = jnp.bfloat16


def tile_of(extent, most):
    return max(t for t in range(128, most + 1, 128) if extent % t == 0)


def rms_scale(values, gain_row):
    mean_sq = jnp.mean(values * values, axis=-1, keepdims=True)
    return values * lax.rsqrt(mean_sq + EPSILON) * gain_row


def iota(shape, axis):
    return lax.broadcasted_iota(jnp.int32, shape, axis)


def dot(a, b):
    return jnp.dot(a, b, preferred_element_type=F32)


def split_pair(values):
    high = values.astype(BF16).astype(F32)
    return jnp.concatenate([high, values - high], axis=1)


def tick(
    sections,
    n,
    stream,
    mixer_gain,
    ssm_weight,
    decay_rate,
    skip_gain,
    mixed_gain,
    ffn_gain,
    router_weight,
    expert_ids,
    gate_hbm,
    up_hbm,
    down_hbm,
    out_ref,
    gate,
    up,
    down,
    local_out,
    local_in,
    decay_out,
    decay_in,
    start_out,
    start_in,
    mixed,
    carry,
    resid,
    notes,
    resid_in,
    notes_in,
    packed,
    arrived,
    rows_in,
    hidden,
    answers,
    shared_in,
    totals,
    answers_in,
    picked,
    w_sem,
    local_send,
    local_recv,
    decay_send,
    decay_recv,
    start_send,
    start_recv,
    pass_send,
    pass_recv,
    rows_send,
    rows_recv,
    share_send,
    share_recv,
    ans_send,
    ans_recv,
):
    sec = lax.axis_index("section")
    me = lax.axis_index("wide")
    after = lax.rem(sec + 1, sections)
    before = lax.rem(sec + sections - 1, sections)
    tok, width = stream.shape
    heads = decay_rate.shape[1]
    head_dim = width // heads
    assert tok == head_dim
    chans = width // n
    members = n // EXPERTS
    my_expert, my_part = me // members, lax.rem(me, members)
    hid = gate.shape[1]
    order = [0]
    for k in range(1, n // 2 + 1):
        order += [k] if 2 * k == n else [k, n - k]

    def wide_at(shift):
        return lax.rem(me + (shift + n), n)

    mates = [
        my_expert,
        my_expert + 1 - 2 * lax.rem(my_expert, 2),
        lax.rem(my_expert + 2, EXPERTS),
        EXPERTS - 1 - my_expert,
    ]

    def peer(q, part_shift):
        return mates[q] * members + lax.rem(my_part + (part_shift + members), members)

    def remote(src, dst, send, recv, section, wide):
        return pltpu.make_async_remote_copy(
            src_ref=src,
            dst_ref=dst,
            send_sem=send,
            recv_sem=recv,
            device_id={"section": section, "wide": wide},
            device_id_type=pl.DeviceIdType.MESH,
        )

    barrier = pltpu.get_barrier_semaphore()
    for k in range(n):
        w = wide_at(k)
        if k:
            pl.semaphore_signal(
                barrier, inc=1, device_id={"section": sec, "wide": w},
                device_id_type=pl.DeviceIdType.MESH,
            )
        for other in (after, before):
            pl.semaphore_signal(
                barrier, inc=1, device_id={"section": other, "wide": w},
                device_id_type=pl.DeviceIdType.MESH,
            )

    weight_copies = []
    for i, (src, dst) in enumerate(((gate_hbm, gate), (up_hbm, up), (down_hbm, down))):
        step = src.shape[0] // PIECES
        weight_copies.append(
            [
                pltpu.make_async_copy(
                    src.at[pl.ds(k * step, step)], dst.at[pl.ds(k * step, step)], w_sem.at[i, k]
                )
                for k in range(PIECES)
            ]
        )
        for copy in weight_copies[-1]:
            copy.start()

    x_in = stream[...].astype(F32)
    normed = rms_scale(x_in, mixer_gain[...]).astype(BF16)
    projected = lax.dot_general(
        normed, ssm_weight[...], (((1,), (1,)), ((), ())), preferred_element_type=F32
    )
    raw = projected[:, 2 * STATE :]
    step_size = jnp.maximum(raw, 0.0) + jnp.log1p(jnp.exp(-jnp.abs(raw)))
    b_rows = projected[:, :STATE] * (1.0 / STATE)
    c_rows = (projected[:, STATE : 2 * STATE] * (1.0 / math.sqrt(STATE))).astype(BF16)
    tri = (iota((tok, tok), 0) >= iota((tok, tok), 1)).astype(BF16)
    steps = split_pair(step_size)
    run = dot(tri, steps.astype(BF16))
    rated = (run[:, :heads] + run[:, heads:]) * decay_rate[...]
    skips = jnp.broadcast_to(split_pair(skip_gain[...]), (16, 2 * heads))
    spread = (
        lax.rem(iota((2 * heads, width), 0), heads) == iota((2 * heads, width), 1) // head_dim
    ).astype(BF16)
    cols = dot(
        jnp.concatenate([steps, split_pair(rated), skips], axis=0).astype(BF16), spread
    )
    step_cols, rated_cols = cols[:tok], cols[tok : 2 * tok]
    skip_cols = cols[2 * tok : 2 * tok + 1]
    values = normed.astype(F32)
    scaled = values * step_cols
    last = rated_cols[tok - 1 : tok]

    b_across = jnp.transpose(b_rows).astype(BF16)
    added = dot(b_across, (scaled * jnp.exp(rated_cols - last)).astype(BF16)).astype(BF16)
    faded = jnp.exp(-last)
    for j in range(n):
        at = slice(j * chans, (j + 1) * chans)
        local_out[j] = added[:, at]
        decay_out[j] = faded[:, at]
    pl.semaphore_wait(barrier, 3 * n - 1)
    own_copies = [
        pltpu.make_async_copy(local_out.at[me], local_in.at[me], local_recv.at[me]),
        pltpu.make_async_copy(decay_out.at[me], decay_in.at[me], decay_recv.at[me]),
    ]
    for copy in own_copies:
        copy.start()
    for p in reversed(range(1, n)):
        w = wide_at(order[p])
        remote(
            decay_out.at[w], decay_in.at[me], decay_send.at[w], decay_recv.at[me], sec, w
        ).start()
        remote(
            local_out.at[w], local_in.at[me], local_send.at[w], local_recv.at[me], sec, w
        ).start()

    per = 256 // head_dim
    block = per * head_dim
    b_short = b_rows.astype(BF16)
    overlap = lax.dot_general(
        c_rows, jnp.concatenate([b_rows] * per, axis=0).astype(BF16),
        (((1,), (1,)), ((), ())), preferred_element_type=F32,
    )
    lane_tok = lax.rem(iota((tok, block), 1), tok)
    lane_head = iota((tok, block), 1) // head_dim
    row_tok = iota((tok, block), 0)
    for g in range(width // block):
        at = slice(g * block, (g + 1) * block)
        rated_g, scaled_g = rated_cols[:, at], scaled[:, at]
        rated_row = jnp.sum(
            jnp.where(row_tok == lane_tok, rated_g, 0.0), axis=0, keepdims=True
        )
        gap = jnp.where(row_tok >= lane_tok, rated_row - rated_g, -1e30)
        mixing = (overlap * jnp.exp(gap)).astype(BF16)
        stacked = jnp.concatenate(
            [jnp.where(lane_head == k, scaled_g, 0.0) for k in range(per)], axis=0
        ).astype(BF16)
        mixed[:, at] = dot(mixing, stacked) + values[:, at] * skip_cols[:, at]
        carry[:, at] = jnp.exp(-rated_g)

    for copy in own_copies:
        copy.wait()
    for p in range(1, n):
        w = wide_at(order[p])
        remote(
            decay_out.at[w], decay_in.at[w], decay_send.at[w], decay_recv.at[w], sec, w
        ).wait()
        remote(
            local_out.at[w], local_in.at[w], local_send.at[w], local_recv.at[w], sec, w
        ).wait()
    state = jnp.zeros((STATE, chans), F32)
    for w in range(n):
        start_out[w] = state.astype(BF16)
        state = state * decay_in[w] + local_in[w].astype(F32)
    start_own = pltpu.make_async_copy(start_out.at[me], start_in.at[me], start_recv.at[me])
    start_own.start()
    for p in reversed(range(1, n)):
        w = wide_at(order[p])
        remote(
            start_out.at[w], start_in.at[me], start_send.at[w], start_recv.at[me], sec, w
        ).start()

    id_rows = jnp.concatenate([expert_ids[...], jnp.zeros((6, tok), jnp.int32)], axis=0)
    ids = jnp.transpose(id_rows.astype(F32)).astype(jnp.int32)
    id0, id1 = ids[:, 0:1], ids[:, 1:2]
    lane = iota((tok, 128), 1)
    chosen = ((lane == id0) | (lane == id1)).astype(BF16)
    earlier = (iota((tok, tok), 0) > iota((tok, tok), 1)).astype(BF16)
    running = dot(earlier, chosen)
    slot0 = jnp.sum(jnp.where(lane == id0, running, 0.0), axis=1, keepdims=True)
    slot1 = jnp.sum(jnp.where(lane == id1, running, 0.0), axis=1, keepdims=True)
    target0 = id0.astype(F32) * CAP + slot0
    target1 = id1.astype(F32) * CAP + slot1
    places = iota((tok, 256), 1).astype(F32)
    placing = jnp.transpose(((places == target0) | (places == target1)).astype(F32)).astype(BF16)

    start_own.wait()
    for p in range(1, n):
        w = wide_at(order[p])
        remote(
            start_out.at[w], start_in.at[w], start_send.at[w], start_recv.at[w], sec, w
        ).wait()
    for j in range(n):
        at = slice(j * chans, (j + 1) * chans)
        mixed[:, at] = mixed[:, at] + dot(c_rows, start_in[j]) * carry[:, at]
    residual = x_in + rms_scale(mixed[...], mixed_gain[...])
    routed = rms_scale(residual, ffn_gain[...]).astype(BF16)
    sent = dot(placing[: EXPERTS * CAP], routed)
    piece = width // CUTS
    for e in range(EXPERTS):
        for c in range(CUTS):
            packed[e, c] = sent[
                e * CAP : (e + 1) * CAP, c * piece : (c + 1) * piece
            ].astype(BF16)

    row_copies = {}
    rows_own = []
    for c in range(CUTS):
        rows_own.append(
            pltpu.make_async_copy(packed.at[my_expert, c], arrived.at[0, c], rows_recv.at[0, c])
        )
        rows_own[-1].start()

    def hand_on(q, c):
        source = arrived.at[q, c] if q else packed.at[my_expert, c]
        for k in range(1, members):
            p = k * EXPERTS + q
            row_copies[p, c] = remote(
                source, arrived.at[p, c], rows_send.at[p, c], rows_recv.at[p, c], sec, peer(0, -k)
            )
            row_copies[p, c].start()

    for c in range(CUTS):
        hand_on(0, c)
    for q in (2, 3, 1):
        for c in range(CUTS):
            row_copies[q, c] = remote(
                packed.at[mates[q], c], arrived.at[q, c], rows_send.at[q, c], rows_recv.at[q, c],
                sec, peer(q, 0),
            )
            row_copies[q, c].start()

    logits = lax.dot_general(
        routed, router_weight[...], (((1,), (1,)), ((), ())), preferred_element_type=F32
    )
    choice = iota((tok, EXPERTS), 1)
    logit0 = jnp.sum(jnp.where(choice == id0, logits, 0.0), axis=1, keepdims=True)
    logit1 = jnp.sum(jnp.where(choice == id1, logits, 0.0), axis=1, keepdims=True)
    share0 = jax.nn.sigmoid(logit0 - logit1)
    resid[...] = residual
    notes[...] = jnp.where(
        lane == 0, target0, jnp.where(lane == 1, target1, jnp.where(lane == 2, share0, 0.0))
    )
    passes = [
        remote(resid, resid_in, pass_send.at[0], pass_recv.at[0], after, me),
        remote(notes, notes_in, pass_send.at[1], pass_recv.at[1], after, me),
    ]
    for copy in passes:
        copy.start()

    def relay(q):
        for c in range(CUTS):
            row_copies[q, c].wait_recv()
            hand_on(q, c)

    hid_tile = tile_of(hid, 512)
    out_tile = totals.shape[3]
    tiles = width // out_tile
    steps_up = hid // hid_tile
    groups = ((0, 2), (1, 3))
    half = n // 2
    share_copies = {}
    answer_copies = {}

    def gather(group):
        block_at = 0
        for k in range(members):
            for q in groups[group]:
                p = k * EXPERTS + q
                for c in range(CUTS):
                    if p == 0:
                        rows_own[c].wait()
                    elif k:
                        row_copies[p, c].wait_recv()
                block_at += 1
            lead = k * EXPERTS + groups[group][0]
            other = k * EXPERTS + groups[group][1]
            top = k * 2 * CAP
            for c in range(CUTS):
                rows_in[top : top + 2 * CAP, c * piece : (c + 1) * piece] = jnp.concatenate(
                    [arrived[lead, c].astype(F32), arrived[other, c].astype(F32)], axis=0
                ).astype(BF16)

    def widen(first, last_step):
        @pl.loop(first, last_step)
        def _(i):
            at = pl.ds(pl.multiple_of(i * hid_tile, hid_tile), hid_tile)
            gate_pre = dot(rows_in[...], gate[:, at])
            up_pre = dot(rows_in[...], up[:, at])
            hidden[:, at] = (gate_pre * jax.nn.sigmoid(gate_pre) * up_pre).astype(BF16)

    def narrow(group):
        for i in range(tiles):
            result = dot(hidden[...], down[:, i * out_tile : (i + 1) * out_tile])
            for k in reversed(range(members)):
                for h, q in enumerate(groups[group]):
                    p = k * EXPERTS + q
                    top = (k * 2 + h) * CAP
                    answers[p, i] = result[top : top + CAP].astype(BF16)
            for k in range(1, members):
                for q in groups[group]:
                    p = k * EXPERTS + q
                    share_copies[p, i] = remote(
                        answers.at[p, i], shared_in.at[p - EXPERTS, i],
                        share_send.at[p - EXPERTS, i], share_recv.at[p - EXPERTS, i],
                        sec, peer(0, k),
                    )
                    share_copies[p, i].start()

    def settle(group, i):
        for q in reversed(groups[group]):
            total = answers[q, i].astype(F32)
            for k in range(1, members):
                p = k * EXPERTS + q
                share_copies[p, i].wait_recv()
                total = total + shared_in[p - EXPERTS, i].astype(F32)
            totals[q, i] = total.astype(BF16)
            answer_copies[q, i] = remote(
                totals.at[q, i], answers_in.at[q, i], ans_send.at[q, i], ans_recv.at[q, i],
                after, peer(q, 0),
            )
            answer_copies[q, i].start()

    relay(2)
    relay(1)
    gather(0)
    for copies in weight_copies[:2]:
        for copy in copies:
            copy.wait()
    cut = steps_up - steps_up // 4
    widen(0, cut)
    relay(3)
    widen(cut, steps_up)
    for copy in weight_copies[2]:
        copy.wait()
    narrow(0)
    gather(1)
    cut = steps_up // 2
    widen(0, cut)
    for i in range(tiles):
        settle(0, i)
    widen(cut, steps_up)
    narrow(1)

    for copy in passes:
        copy.wait()
    told = notes_in[...]
    goal0, goal1, first_share = told[:, 0:1], told[:, 1:2], told[:, 2:3]
    slot_lane = iota((tok, CAP), 1)

    def take(q):
        spots = (slot_lane + mates[q] * CAP).astype(F32)
        return jnp.concatenate(
            [(spots == goal0).astype(F32), (spots == goal1).astype(F32)], axis=0
        ).astype(BF16)

    for i in range(tiles):
        settle(1, i)
    takes = [take(q) for q in range(EXPERTS)]
    for i in range(tiles):
        at = slice(i * out_tile, (i + 1) * out_tile)
        found = None
        for q in groups[0]:
            answer_copies[q, i].wait_recv()
            part = dot(takes[q], answers_in[q, i])
            found = part if found is None else found + part
        picked[:, at] = found
    for i in range(tiles):
        at = slice(i * out_tile, (i + 1) * out_tile)
        found = picked[:, at]
        for q in groups[1]:
            answer_copies[q, i].wait_recv()
            found = found + dot(takes[q], answers_in[q, i])
        out_ref[:, at] = (
            resid_in[:, at] + (first_share * found[:tok] + (1.0 - first_share) * found[tok:])
        ).astype(BF16)
    for p in range(1, n):
        for c in range(CUTS):
            row_copies[p, c].wait_send()
    for copy in share_copies.values():
        copy.wait_send()
    for copy in answer_copies.values():
        copy.wait_send()


def local(
    stream,
    mixer_gain,
    ssm_weight,
    decay_rate,
    skip_gain,
    mixed_gain,
    ffn_gain,
    router_weight,
    expert_ids,
    gate_weight,
    up_weight,
    down_weight,
):
    n = lax.axis_size("wide")
    sections = lax.axis_size("section")
    _, tok, width = stream.shape
    hid = gate_weight.shape[2]
    chans = width // n
    out_tile = tile_of(width, 512)
    tiles = width // out_tile
    dma = pltpu.SemaphoreType.DMA
    vmem = pl.BlockSpec(memory_space=pltpu.VMEM)
    hbm = pl.BlockSpec(memory_space=pl.ANY)
    result = pl.pallas_call(
        functools.partial(tick, sections, n),
        out_shape=jax.ShapeDtypeStruct((tok, width), BF16),
        in_specs=[vmem] * 9 + [hbm] * 3,
        out_specs=vmem,
        scratch_shapes=[
            pltpu.VMEM((width, hid), BF16),
            pltpu.VMEM((width, hid), BF16),
            pltpu.VMEM((hid, width), BF16),
            pltpu.VMEM((n, STATE, chans), BF16),
            pltpu.VMEM((n, STATE, chans), BF16),
            pltpu.VMEM((n, 1, chans), F32),
            pltpu.VMEM((n, 1, chans), F32),
            pltpu.VMEM((n, STATE, chans), BF16),
            pltpu.VMEM((n, STATE, chans), BF16),
            pltpu.VMEM((tok, width), F32),
            pltpu.VMEM((tok, width), F32),
            pltpu.VMEM((tok, width), F32),
            pltpu.VMEM((tok, 128), F32),
            pltpu.VMEM((tok, width), F32),
            pltpu.VMEM((tok, 128), F32),
            pltpu.VMEM((EXPERTS, CUTS, CAP, width // CUTS), BF16),
            pltpu.VMEM((n, CUTS, CAP, width // CUTS), BF16),
            pltpu.VMEM((n // 2 * CAP, width), BF16),
            pltpu.VMEM((n // 2 * CAP, hid), BF16),
            pltpu.VMEM((n, tiles, CAP, out_tile), BF16),
            pltpu.VMEM((n - EXPERTS, tiles, CAP, out_tile), BF16),
            pltpu.VMEM((EXPERTS, tiles, CAP, out_tile), BF16),
            pltpu.VMEM((EXPERTS, tiles, CAP, out_tile), BF16),
            pltpu.VMEM((2 * tok, width), F32),
            dma((3, PIECES)),
            dma((n,)),
            dma((n,)),
            dma((n,)),
            dma((n,)),
            dma((n,)),
            dma((n,)),
            dma((2,)),
            dma((2,)),
            dma((n, CUTS)),
            dma((n, CUTS)),
            dma((n - EXPERTS, tiles)),
            dma((n - EXPERTS, tiles)),
            dma((EXPERTS, tiles)),
            dma((EXPERTS, tiles)),
        ],
        compiler_params=pltpu.CompilerParams(
            collective_id=0, has_side_effects=True, vmem_limit_bytes=VMEM_BYTES
        ),
    )(
        stream[0],
        mixer_gain,
        ssm_weight[0].T,
        decay_rate,
        skip_gain,
        mixed_gain,
        ffn_gain,
        router_weight[0].T,
        expert_ids[0].T,
        gate_weight[0],
        up_weight[0],
        down_weight[0],
    )
    return result[None]


def solution(mesh):
    return jax.shard_map(
        local,
        mesh=mesh,
        in_specs=(
            P("section", "wide", None),
            P("section", None),
            P("section", None, None),
            P("section", None),
            P("section", None),
            P("section", None),
            P("section", None),
            P("section", None, None),
            P("section", "wide", None),
            P("section", None, "wide"),
            P("section", None, "wide"),
            P("section", "wide", None),
        ),
        out_specs=P("section", "wide", None),
        check_vma=False,
    )
```

time: 84.5 us -> 76.5 us (0.905); the launches traced: 82.8 us -> 76.3 us
  Pallas kernels: 81.1 us -> 74.7 us
    pallas_call x1, Pallas kernels: 81.1 us -> 74.7 us  [local(): pl.pallas_call(functools.partial(tick, sections, n), out_shape=jax.ShapeD...]
where the time goes in v1:
time: 76.5 us; the launch traced here: 76.3 us
  Pallas kernels  74.7 us (98%)
  local copies, waits for them, and re-layouts  1.67 us (2%)
    pallas_call x1, Pallas kernels, local(): pl.pallas_call(functools.partial(tick, sections, n), out_shape=jax.ShapeD...  74.7 us
    unnamed x1, local copies, waits for them, and re-layouts  1.67 us

profile of v1, /device:TPU:1, one launch (start us, length us, event | category | flops | bytes accessed | tf_op | source)
XLA Modules:
  0.0 76.3 jit_solution(194298527901242096)
XLA Ops:
  0.0 74.7 %shard_map.118 = bf16[64,2048]{1,0:T(8,128)(2,1)} custom-call(bf16[64,2048]{1,0:T(8,128)(2,1)} %bitcast.19, f32[1,2048]{1,0:T(1,128)} %mixer_gain.1, bf16[160,2048]{1,0:T(8,128)(2,1)} %bitcast.18, f32[1,32]{1,0:T(1,128)} %decay_rate.1, f32[1,32]{1,0:T(1,128)} %skip_gain.1, f32[1,2048]{1,0:T(1,128)} %mixed_gain.1, f32[1,2048]{1,0:T(1,128)} %ffn_gain.1, ...), custom_call_target="tpu_custom_call" | custom-call | tf_op jit(solution)/shard_map/pallas_call | solution.py:499
  74.7 1.7 %copy.14 = bf16[1,64,2048]{2,1,0:T(8,128)(2,1)} copy(bf16[1,64,2048]{2,1,0:T(8,128)(2,1)} %bitcast.17) | data formatting | bytes 524288

commit v2 on v1

--- a/solution.py
+++ b/solution.py
@@ -14,6 +14,7 @@
 EPSILON = 1e-05
 PIECES = 8
 CUTS = 2
+LAYERS = 2
 VMEM_BYTES = 67_000_000
 F32 = jnp.float32
 BF16 = jnp.bfloat16
@@ -193,25 +194,39 @@
     b_across = jnp.transpose(b_rows).astype(BF16)
     added = dot(b_across, (scaled * jnp.exp(rated_cols - last)).astype(BF16)).astype(BF16)
     faded = jnp.exp(-last)
+    depth = STATE // LAYERS
     for j in range(n):
         at = slice(j * chans, (j + 1) * chans)
-        local_out[j] = added[:, at]
         decay_out[j] = faded[:, at]
+        for s in range(LAYERS):
+            local_out[s, j] = added[s * depth : (s + 1) * depth, at]
     pl.semaphore_wait(barrier, 3 * n - 1)
-    own_copies = [
-        pltpu.make_async_copy(local_out.at[me], local_in.at[me], local_recv.at[me]),
-        pltpu.make_async_copy(decay_out.at[me], decay_in.at[me], decay_recv.at[me]),
-    ]
-    for copy in own_copies:
-        copy.start()
+    decay_own = pltpu.make_async_copy(decay_out.at[me], decay_in.at[me], decay_recv.at[me])
+    decay_own.start()
     for p in reversed(range(1, n)):
         w = wide_at(order[p])
         remote(
             decay_out.at[w], decay_in.at[me], decay_send.at[w], decay_recv.at[me], sec, w
         ).start()
-        remote(
-            local_out.at[w], local_in.at[me], local_send.at[w], local_recv.at[me], sec, w
-        ).start()
+
+    def spread_out(s, source, target, send, recv):
+        pltpu.make_async_copy(source.at[s, me], target.at[s, me], recv.at[s, me]).start()
+        for p in reversed(range(1, n)):
+            w = wide_at(order[p])
+            remote(
+                source.at[s, w], target.at[s, me], send.at[s, w], recv.at[s, me], sec, w
+            ).start()
+
+    def collect(s, source, target, send, recv):
+        pltpu.make_async_copy(source.at[s, me], target.at[s, me], recv.at[s, me]).wait()
+        for p in range(1, n):
+            w = wide_at(order[p])
+            remote(
+                source.at[s, w], target.at[s, w], send.at[s, w], recv.at[s, w], sec, w
+            ).wait()
+
+    for s in range(LAYERS):
+        spread_out(s, local_out, local_in, local_send, local_recv)
 
     per = 256 // head_dim
     block = per * head_dim
@@ -237,27 +252,19 @@
         mixed[:, at] = dot(mixing, stacked) + values[:, at] * skip_cols[:, at]
         carry[:, at] = jnp.exp(-rated_g)
 
-    for copy in own_copies:
-        copy.wait()
+    decay_own.wait()
     for p in range(1, n):
         w = wide_at(order[p])
         remote(
             decay_out.at[w], decay_in.at[w], decay_send.at[w], decay_recv.at[w], sec, w
         ).wait()
-        remote(
-            local_out.at[w], local_in.at[w], local_send.at[w], local_recv.at[w], sec, w
-        ).wait()
-    state = jnp.zeros((STATE, chans), F32)
-    for w in range(n):
-        start_out[w] = state.astype(BF16)
-        state = state * decay_in[w] + local_in[w].astype(F32)
-    start_own = pltpu.make_async_copy(start_out.at[me], start_in.at[me], start_recv.at[me])
-    start_own.start()
-    for p in reversed(range(1, n)):
-        w = wide_at(order[p])
-        remote(
-            start_out.at[w], start_in.at[me], start_send.at[w], start_recv.at[me], sec, w
-        ).start()
+    for s in range(LAYERS):
+        collect(s, local_out, local_in, local_send, local_recv)
+        state = jnp.zeros((depth, chans), F32)
+        for w in range(n):
+            start_out[s, w] = state.astype(BF16)
+            state = state * decay_in[w] + local_in[s, w].astype(F32)
+        spread_out(s, start_out, start_in, start_send, start_recv)
 
     id_rows = jnp.concatenate([expert_ids[...], jnp.zeros((6, tok), jnp.int32)], axis=0)
     ids = jnp.transpose(id_rows.astype(F32)).astype(jnp.int32)
@@ -273,15 +280,12 @@
     places = iota((tok, 256), 1).astype(F32)
     placing = jnp.transpose(((places == target0) | (places == target1)).astype(F32)).astype(BF16)
 
-    start_own.wait()
-    for p in range(1, n):
-        w = wide_at(order[p])
-        remote(
-            start_out.at[w], start_in.at[w], start_send.at[w], start_recv.at[w], sec, w
-        ).wait()
+    for s in range(LAYERS):
+        collect(s, start_out, start_in, start_send, start_recv)
     for j in range(n):
         at = slice(j * chans, (j + 1) * chans)
-        mixed[:, at] = mixed[:, at] + dot(c_rows, start_in[j]) * carry[:, at]
+        begun = jnp.concatenate([start_in[s, j] for s in range(LAYERS)], axis=0)
+        mixed[:, at] = mixed[:, at] + dot(c_rows, begun) * carry[:, at]
     residual = x_in + rms_scale(mixed[...], mixed_gain[...])
     routed = rms_scale(residual, ffn_gain[...]).astype(BF16)
     sent = dot(placing[: EXPERTS * CAP], routed)
@@ -311,7 +315,7 @@
 
     for c in range(CUTS):
         hand_on(0, c)
-    for q in (2, 3, 1):
+    for q in (2, 1, 3):
         for c in range(CUTS):
             row_copies[q, c] = remote(
                 packed.at[mates[q], c], arrived.at[q, c], rows_send.at[q, c], rows_recv.at[q, c],
@@ -337,10 +341,9 @@
     for copy in passes:
         copy.start()
 
-    def relay(q):
-        for c in range(CUTS):
-            row_copies[q, c].wait_recv()
-            hand_on(q, c)
+    def relay(q, c):
+        row_copies[q, c].wait_recv()
+        hand_on(q, c)
 
     hid_tile = tile_of(hid, 512)
     out_tile = totals.shape[3]
@@ -370,13 +373,24 @@
                     [arrived[lead, c].astype(F32), arrived[other, c].astype(F32)], axis=0
                 ).astype(BF16)
 
-    def widen(first, last_step):
-        @pl.loop(first, last_step)
+    def widen_span(first, beyond):
+        @pl.loop(first, beyond)
         def _(i):
             at = pl.ds(pl.multiple_of(i * hid_tile, hid_tile), hid_tile)
             gate_pre = dot(rows_in[...], gate[:, at])
             up_pre = dot(rows_in[...], up[:, at])
             hidden[:, at] = (gate_pre * jax.nn.sigmoid(gate_pre) * up_pre).astype(BF16)
+
+    def widen(hooks):
+        done = 0
+        for share, action in hooks:
+            upto = int(steps_up * share)
+            if upto > done:
+                widen_span(done, upto)
+            action()
+            done = max(done, upto)
+        if done < steps_up:
+            widen_span(done, steps_up)
 
     def narrow(group):
         for i in range(tiles):
@@ -410,25 +424,19 @@
             )
             answer_copies[q, i].start()
 
-    relay(2)
-    relay(1)
+    for q in (2, 1):
+        for c in range(CUTS):
+            relay(q, c)
     gather(0)
     for copies in weight_copies[:2]:
         for copy in copies:
             copy.wait()
-    cut = steps_up - steps_up // 4
-    widen(0, cut)
-    relay(3)
-    widen(cut, steps_up)
+    widen([((2 + c) / (2 + CUTS), functools.partial(relay, 3, c)) for c in range(CUTS)])
     for copy in weight_copies[2]:
         copy.wait()
     narrow(0)
     gather(1)
-    cut = steps_up // 2
-    widen(0, cut)
-    for i in range(tiles):
-        settle(0, i)
-    widen(cut, steps_up)
+    widen([((2 + 2 * i / (tiles - 1)) / 4, functools.partial(settle, 0, i)) for i in range(tiles)])
     narrow(1)
 
     for copy in passes:
@@ -505,12 +513,12 @@
             pltpu.VMEM((width, hid), BF16),
             pltpu.VMEM((width, hid), BF16),
             pltpu.VMEM((hid, width), BF16),
-            pltpu.VMEM((n, STATE, chans), BF16),
-            pltpu.VMEM((n, STATE, chans), BF16),
+            pltpu.VMEM((LAYERS, n, STATE // LAYERS, chans), BF16),
+            pltpu.VMEM((LAYERS, n, STATE // LAYERS, chans), BF16),
             pltpu.VMEM((n, 1, chans), F32),
             pltpu.VMEM((n, 1, chans), F32),
-            pltpu.VMEM((n, STATE, chans), BF16),
-            pltpu.VMEM((n, STATE, chans), BF16),
+            pltpu.VMEM((LAYERS, n, STATE // LAYERS, chans), BF16),
+            pltpu.VMEM((LAYERS, n, STATE // LAYERS, chans), BF16),
             pltpu.VMEM((tok, width), F32),
             pltpu.VMEM((tok, width), F32),
             pltpu.VMEM((tok, width), F32),
@@ -527,12 +535,12 @@
             pltpu.VMEM((EXPERTS, tiles, CAP, out_tile), BF16),
             pltpu.VMEM((2 * tok, width), F32),
             dma((3, PIECES)),
+            dma((LAYERS, n)),
+            dma((LAYERS, n)),
             dma((n,)),
             dma((n,)),
-            dma((n,)),
-            dma((n,)),
-            dma((n,)),
-            dma((n,)),
+            dma((LAYERS, n)),
+            dma((LAYERS, n)),
             dma((2,)),
             dma((2,)),
             dma((n, CUTS)),

time: 76.5 us -> 66.8 us (0.87)
  Pallas kernels: 74.7 us -> 65 us
    pallas_call x1, Pallas kernels: 74.7 us -> 65 us  [local(): pl.pallas_call(functools.partial(tick, sections, n), out_shape=jax.ShapeD...]
where the time goes in v2:
time: 66.8 us; the launch traced here: 66.7 us
  Pallas kernels  65 us (97%)
  local copies, waits for them, and re-layouts  1.67 us (2%)
    pallas_call x1, Pallas kernels, local(): pl.pallas_call(functools.partial(tick, sections, n), out_shape=jax.ShapeD...  65 us
    unnamed x1, local copies, waits for them, and re-layouts  1.67 us

profile of v2, /device:TPU:1, one launch (start us, length us, event | category | flops | bytes accessed | tf_op | source)
XLA Modules:
  0.0 66.7 jit_solution(11879753174729828109)
XLA Ops:
  0.0 65.0 %shard_map.118 = bf16[64,2048]{1,0:T(8,128)(2,1)} custom-call(bf16[64,2048]{1,0:T(8,128)(2,1)} %bitcast.19, f32[1,2048]{1,0:T(1,128)} %mixer_gain.1, bf16[160,2048]{1,0:T(8,128)(2,1)} %bitcast.18, f32[1,32]{1,0:T(1,128)} %decay_rate.1, f32[1,32]{1,0:T(1,128)} %skip_gain.1, f32[1,2048]{1,0:T(1,128)} %mixed_gain.1, f32[1,2048]{1,0:T(1,128)} %ffn_gain.1, ...), custom_call_target="tpu_custom_call" | custom-call | tf_op jit(solution)/shard_map/pallas_call | solution.py:507
  65.0 1.7 %copy.14 = bf16[1,64,2048]{2,1,0:T(8,128)(2,1)} copy(bf16[1,64,2048]{2,1,0:T(8,128)(2,1)} %bitcast.17) | data formatting | bytes 524288

commit v3 on v2

--- a/solution.py
+++ b/solution.py
@@ -82,6 +82,7 @@
     totals,
     answers_in,
     picked,
+    finished,
     w_sem,
     local_send,
     local_recv,
@@ -97,6 +98,7 @@
     share_recv,
     ans_send,
     ans_recv,
+    out_sem,
 ):
     sec = lax.axis_index("section")
     me = lax.axis_index("wide")
@@ -462,15 +464,20 @@
             part = dot(takes[q], answers_in[q, i])
             found = part if found is None else found + part
         picked[:, at] = found
+    out_copies = []
     for i in range(tiles):
         at = slice(i * out_tile, (i + 1) * out_tile)
         found = picked[:, at]
         for q in groups[1]:
             answer_copies[q, i].wait_recv()
             found = found + dot(takes[q], answers_in[q, i])
-        out_ref[:, at] = (
+        finished[:, at] = (
             resid_in[:, at] + (first_share * found[:tok] + (1.0 - first_share) * found[tok:])
         ).astype(BF16)
+        out_copies.append(
+            pltpu.make_async_copy(finished.at[:, at], out_ref.at[:, at], out_sem.at[i])
+        )
+        out_copies[-1].start()
     for p in range(1, n):
         for c in range(CUTS):
             row_copies[p, c].wait_send()
@@ -478,6 +485,8 @@
         copy.wait_send()
     for copy in answer_copies.values():
         copy.wait_send()
+    for copy in out_copies:
+        copy.wait()
 
 
 def local(
@@ -508,7 +517,7 @@
         functools.partial(tick, sections, n),
         out_shape=jax.ShapeDtypeStruct((tok, width), BF16),
         in_specs=[vmem] * 9 + [hbm] * 3,
-        out_specs=vmem,
+        out_specs=hbm,
         scratch_shapes=[
             pltpu.VMEM((width, hid), BF16),
             pltpu.VMEM((width, hid), BF16),
@@ -534,6 +543,7 @@
             pltpu.VMEM((EXPERTS, tiles, CAP, out_tile), BF16),
             pltpu.VMEM((EXPERTS, tiles, CAP, out_tile), BF16),
             pltpu.VMEM((2 * tok, width), F32),
+            pltpu.VMEM((tok, width), BF16),
             dma((3, PIECES)),
             dma((LAYERS, n)),
             dma((LAYERS, n)),
@@ -549,6 +559,7 @@
             dma((n - EXPERTS, tiles)),
             dma((EXPERTS, tiles)),
             dma((EXPERTS, tiles)),
+            dma((tiles,)),
         ],
         compiler_params=pltpu.CompilerParams(
             collective_id=0, has_side_effects=True, vmem_limit_bytes=VMEM_BYTES

time: 66.8 us -> 66.7 us (level)
  no operation moved by 1% of the time
where the time goes in v3:
time: 66.7 us; the launch traced here: 66.6 us
  Pallas kernels  64.9 us (97%)
  local copies, waits for them, and re-layouts  1.67 us (3%)
    pallas_call x1, Pallas kernels, local(): pl.pallas_call(functools.partial(tick, sections, n), out_shape=jax.ShapeD...  64.9 us
    unnamed x1, local copies, waits for them, and re-layouts  1.67 us

profile of v3, /device:TPU:1, one launch (start us, length us, event | category | flops | bytes accessed | tf_op | source)
XLA Modules:
  0.0 66.6 jit_solution(4646173702299477421)
XLA Ops:
  0.0 64.9 %shard_map.118 = bf16[64,2048]{1,0:T(8,128)(2,1)} custom-call(bf16[64,2048]{1,0:T(8,128)(2,1)} %bitcast.19, f32[1,2048]{1,0:T(1,128)} %mixer_gain.1, bf16[160,2048]{1,0:T(8,128)(2,1)} %bitcast.18, f32[1,32]{1,0:T(1,128)} %decay_rate.1, f32[1,32]{1,0:T(1,128)} %skip_gain.1, f32[1,2048]{1,0:T(1,128)} %mixed_gain.1, f32[1,2048]{1,0:T(1,128)} %ffn_gain.1, ...), custom_call_target="tpu_custom_call" | custom-call | tf_op jit(solution)/shard_map/pallas_call | solution.py:516
  64.9 1.7 %copy.14 = bf16[1,64,2048]{2,1,0:T(8,128)(2,1)} copy(bf16[1,64,2048]{2,1,0:T(8,128)(2,1)} %bitcast.17) | data formatting | bytes 524288
